TPU v7x, 128 devices: a whole 4x4x4 slice. The times are simulated.
128 devices in a mesh: depth: 2 (over core), row: 16 (over z, x), col: 4 (over y).
Axes of the slice: x: 4, y: 4, z: 4, core: 2. Of those that a mesh axis runs over, the one named last changes fastest.
Arguments:
- right_side: bfloat16 [4, 16, 8, 128, 512], P(None, 'row', ('depth', 'col')), may hold values from -6 to 6
- inverse_diag: bfloat16 [4, 16, 8, 1, 128, 128], P(None, 'row', ('depth', 'col')), may hold values from -2 to 2.5, as said below
- coupling: bfloat16 [3, 16, 1024, 8, 2048], P(None, 'row', None, ('depth', 'col')), may hold values from -0.0625 to 0.0625
- pattern: int32 [3, 16, 8, 8, 16], P(None, 'row', None, ('depth', 'col')), may hold values 0 or 1
Outputs:
- forward_solution: bfloat16 [4, 16, 8, 128, 512], P(None, 'row', ('depth', 'col'))
- solution: bfloat16 [4, 16, 8, 128, 512], P(None, 'row', ('depth', 'col'))
Inputs may be any that keep to these rules, and one draw needn't show every extreme that they name: `inverse_diag`: each block is lower triangular with positive diagonal.
All inputs are finite; a program needn't handle non-finite values. No bound on the sum of `pattern` on one device may be relied on, other than what follows from the above.
Results may differ from a plain program's by a relative error of at most 0.025.
Values may be sent and summed in bfloat16 or wider, within the bound.
A program may use at most 128 MiB of HBM per device.

v0:
```python
import jax
import jax.numpy as jnp
from jax import lax
from jax.sharding import PartitionSpec as P


def apply_inverse(inverse, vector, transposed):
    blocks_in = vector.reshape(inverse.shape[0], inverse.shape[1], vector.shape[-1])
    einsum_form = "tji,tjn->tin" if transposed else "tij,tjn->tin"
    result = jnp.einsum(einsum_form, inverse, blocks_in, preferred_element_type=jnp.float32)
    return result.astype(jnp.bfloat16).reshape(vector.shape)


def lift_upward(masked, share_in):
    portion = lax.all_gather(share_in, "row", axis=0, tiled=True)
    span_rows = portion.shape[0] * portion.shape[2]
    return jnp.dot(
        masked, portion.reshape(span_rows, portion.shape[-1]), preferred_element_type=jnp.float32
    )


def carry_downward(masked, share_in):
    portion = lax.all_gather(share_in, ("depth", "col"), axis=1, tiled=True)
    span_rows = portion.shape[1] * portion.shape[2]
    return lax.dot_general(
        masked,
        portion.reshape(span_rows, portion.shape[-1]),
        (((0,), (0,)), ((), ())),
        preferred_element_type=jnp.float32,
    )


def forward_sum(partial_value, share_rows):
    blocks = partial_value.reshape(
        lax.axis_size(("depth", "col")), share_rows, partial_value.shape[-1]
    )
    summed = lax.psum(blocks.astype(jnp.bfloat16), ("depth", "col")).astype(jnp.float32)
    return lax.dynamic_index_in_dim(summed, lax.axis_index(("depth", "col")), 0, keepdims=False)


def backward_sum(partial_value, share_rows):
    blocks = partial_value.reshape(lax.axis_size("row"), share_rows, partial_value.shape[-1])
    summed = lax.psum(blocks.astype(jnp.bfloat16), "row").astype(jnp.float32)
    return lax.dynamic_index_in_dim(summed, lax.axis_index("row"), 0, keepdims=False)


def body(right_side, inverse_diag, coupling, pattern):
    levels = right_side.shape[0]
    share_rows = right_side.shape[3]
    rhs_cols = right_side.shape[4]
    block_width = inverse_diag.shape[-1]
    masked = []
    for pair_at in range(levels - 1):
        slab = coupling[pair_at, 0, :, 0, :]
        gate = pattern[pair_at, 0, :, 0, :].astype(jnp.bfloat16)
        shaped = (
            slab.reshape(gate.shape[0], block_width, gate.shape[1], block_width)
            * gate[:, None, :, None]
        )
        masked.append(shaped.reshape(slab.shape))
    panel_spans = [(0, rhs_cols)]
    fwd_levels = []
    for level_at in range(levels):
        pieces = []
        for panel_at, (col_first, col_last) in enumerate(panel_spans):
            source = right_side[level_at, 0, 0, :, col_first:col_last]
            if level_at == 0:
                residual = source
            else:
                partial_value = lift_upward(
                    masked[level_at - 1], fwd_levels[level_at - 1][panel_at][None, None]
                )
                residual = (
                    source.astype(jnp.float32) - forward_sum(partial_value, share_rows)
                ).astype(jnp.bfloat16)
            pieces.append(apply_inverse(inverse_diag[level_at, 0, 0], residual, False))
        fwd_levels.append(pieces)
    bwd_levels = [None] * levels
    for level_at in reversed(range(levels)):
        pieces = []
        panel_at = 0
        known_part = fwd_levels[level_at][panel_at]
        if level_at == levels - 1:
            residual = known_part
        else:
            partial_value = carry_downward(
                masked[level_at], bwd_levels[level_at + 1][panel_at][None, None]
            )
            residual = (
                known_part.astype(jnp.float32) - backward_sum(partial_value, share_rows)
            ).astype(jnp.bfloat16)
        pieces.append(apply_inverse(inverse_diag[level_at, 0, 0], residual, True))
        bwd_levels[level_at] = pieces
    forward_rows = []
    backward_rows = []
    for level_at in range(levels):
        forward_rows.append(jnp.concatenate(fwd_levels[level_at], axis=1))
        backward_rows.append(jnp.concatenate(bwd_levels[level_at], axis=1))
    forward_solution = jnp.stack(forward_rows).reshape(levels, 1, 1, share_rows, rhs_cols)
    solution = jnp.stack(backward_rows).reshape(levels, 1, 1, share_rows, rhs_cols)
    return (forward_solution, solution)


def solution(mesh):
    placed = (
        P(None, "row", ("depth", "col"), None, None),
        P(None, "row", ("depth", "col"), None, None, None),
        P(None, "row", None, ("depth", "col"), None),
        P(None, "row", None, ("depth", "col"), None),
    )
    return jax.shard_map(
        body,
        mesh=mesh,
        in_specs=placed,
        out_specs=(
            P(None, "row", ("depth", "col"), None, None),
            P(None, "row", ("depth", "col"), None, None),
        ),
        check_vma=False,
    )
```

profile of v0, /device:TPU:0, one launch (start us, length us, event | category | flops | bytes accessed | tf_op | source)
XLA Modules:
  0.0 735.9 jit_solution(18099699853977080136)
XLA Ops:
  7.2 1.8 convolution_convert_fusion.10
  9.0 0.7 convert.11
  9.8 2.6 mul.62
  12.3 7.3 mul.63
  19.6 2.6 mul.71
  22.2 7.3 mul.72
  29.6 2.6 mul.67
  32.2 7.4 mul.68
  39.5 13.6 %slice_multiply_fusion.2 = (bf16[1,1,1024,1,2048]{4,2,3,1,0:T(8,128)(2,1)}, bf16[1,1,1024,1,2048]{4,2,3,1,0:T(8,128)(2,1)}, bf16[1,1,1024,1,2048]{4,2,3,1,0:T(8,128)(2,1)}) fusion(bf16[1,1,1024,1,2048]{4,2,3,1,0:T(8,128)(2,1)} %mul.63, bf16[3,1,1024,1,2048]{4,2,3,1,0:T(8,128)(2,1)} %param.6, bf16[1,1,1024,1,2048]{4,2,3,1,0:T(8,128)(2,1)} %mul.72, ...), kind=kLoop, calls=%fused_computation.8 | loop fusion | flops 6291456 | bytes 37748736 | tf_op jit(solution)/shard_map/mul | solution.py:57
  53.1 5.1 all-gather.13.cloned.1.call-done
  58.2 6.2 fusion.9
  64.5 62.1 %all-reduce.7.cloned.1.call-done = bf16[8,128,512]{2,1,0:T(8,128)(2,1)} async-done(((bf16[8,128,512]{2,1,0:T(8,128)(2,1)}), bf16[8,128,512]{2,1,0:T(8,128)(2,1)}) %all-reduce.7.cloned.1.call-update) | async-done | bytes 1048592 | tf_op jit(solution)/shard_map/psum | solution.py:37
  126.6 1.7 convolution_convert_fusion.5
  128.4 0.0 all-reduce.9.cloned.1.call-start
  128.5 45.3 %all-gather.15.cloned.1.call-done = bf16[2048,512]{1,0:T(8,128)(2,1)} async-done(((bf16[128,512]{1,0:T(8,128)(2,1)}), bf16[2048,512]{1,0:T(8,128)(2,1)}) %all-gather.15.cloned.1.call-update) | async-done | bytes 2097168 | tf_op jit(solution)/shard_map/all_gather | solution.py:15
  173.7 6.2 fusion.12
  180.0 0.0 all-gather.17.cloned.1.call-start
  180.0 62.1 %all-reduce.9.cloned.1.call-done = bf16[8,128,512]{2,1,0:T(8,128)(2,1)} async-done(((bf16[8,128,512]{2,1,0:T(8,128)(2,1)}), bf16[8,128,512]{2,1,0:T(8,128)(2,1)}) %all-reduce.9.cloned.1.call-update) | async-done | bytes 1048592 | tf_op jit(solution)/shard_map/psum | solution.py:37
  242.1 1.7 convolution_convert_fusion.4
  243.9 0.0 all-reduce.11.cloned.1.call-start
  243.9 44.5 %all-gather.17.cloned.1.call-done = bf16[2048,512]{1,0:T(8,128)(2,1)} async-done(((bf16[128,512]{1,0:T(8,128)(2,1)}), bf16[2048,512]{1,0:T(8,128)(2,1)}) %all-gather.17.cloned.1.call-update) | async-done | bytes 2097168 | tf_op jit(solution)/shard_map/all_gather | solution.py:15
  288.5 6.2 fusion.15
  294.7 0.0 all-gather.19.cloned.1.call-start
  294.7 62.1 %all-reduce.11.cloned.1.call-done = bf16[8,128,512]{2,1,0:T(8,128)(2,1)} async-done(((bf16[8,128,512]{2,1,0:T(8,128)(2,1)}), bf16[8,128,512]{2,1,0:T(8,128)(2,1)}) %all-reduce.11.cloned.1.call-update) | async-done | bytes 1048592 | tf_op jit(solution)/shard_map/psum | solution.py:37
  356.8 1.1 convolution_convert_fusion.3
  357.9 0.9 convolution_convert_fusion.9
  358.8 0.2 all-reduce.13.cloned.1.call-start
  359.0 15.1 %fusion.2 = (bf16[2048,1024]{0,1:T(8,128)(2,1)}, bf16[2048,1024]{0,1:T(8,128)(2,1)}, bf16[2048,1024]{0,1:T(8,128)(2,1)}) fusion(bf16[128,8,16,128]{3,2,1,0:T(8,128)(2,1)} %bitcast.180, bf16[3,1,1024,1,2048]{4,2,3,1,0:T(8,128)(2,1)} %param.6, bf16[128,8,16,128]{3,2,1,0:T(8,128)(2,1)} %bitcast.182, bf16[128,8,16,128]{3,2,1,0:T(8,128)(2,1)} %bitcast.181), kind=kLoop, calls=%fused_computation.5 | loop fusion | flops 6291456 | bytes 37748736 | tf_op jit(solution)/shard_map/dot_general | solution.py:25
  374.1 6.4 copy.26
  380.5 1.1 all-gather.19.cloned.1.call-done
  381.6 6.3 convolution_convert_fusion.2
  387.9 92.3 %all-reduce.13.cloned.1.call-done = bf16[16,128,512]{2,1,0:T(8,128)(2,1)} async-done(((bf16[16,128,512]{2,1,0:T(8,128)(2,1)}), bf16[16,128,512]{2,1,0:T(8,128)(2,1)}) %all-reduce.13.cloned.1.call-update) | async-done | bytes 2097168 | tf_op jit(solution)/shard_map/psum | solution.py:43
  480.2 1.8 convolution_convert_fusion.8
  482.0 0.0 all-reduce.15.cloned.1.call-start
  482.1 6.4 copy.25
  488.5 16.4 %all-gather.21.cloned.1.call-done = bf16[1024,512]{0,1:T(8,128)(2,1)} async-done(((bf16[128,512]{0,1:T(8,128)(2,1)}), bf16[1024,512]{0,1:T(8,128)(2,1)}) %all-gather.21.cloned.1.call-update) | async-done | bytes 1048592 | tf_op jit(solution)/shard_map/all_gather | solution.py:23
  504.9 6.3 convolution_convert_fusion.1
  511.2 92.3 %all-reduce.15.cloned.1.call-done = bf16[16,128,512]{2,1,0:T(8,128)(2,1)} async-done(((bf16[16,128,512]{2,1,0:T(8,128)(2,1)}), bf16[16,128,512]{2,1,0:T(8,128)(2,1)}) %all-reduce.15.cloned.1.call-update) | async-done | bytes 2097168 | tf_op jit(solution)/shard_map/psum | solution.py:43
  603.5 1.8 convolution_convert_fusion.7
  605.3 0.0 all-reduce.17.cloned.1.call-start
  605.3 6.4 copy.24
  611.7 16.4 %all-gather.23.cloned.1.call-done = bf16[1024,512]{0,1:T(8,128)(2,1)} async-done(((bf16[128,512]{0,1:T(8,128)(2,1)}), bf16[1024,512]{0,1:T(8,128)(2,1)}) %all-gather.23.cloned.1.call-update) | async-done | bytes 1048592 | tf_op jit(solution)/shard_map/all_gather | solution.py:23
  628.2 6.3 convolution_convert_fusion
  634.5 0.9 maximum_bitcast_fusion
  635.3 91.5 %all-reduce.17.cloned.1.call-done = bf16[16,128,512]{2,1,0:T(8,128)(2,1)} async-done(((bf16[16,128,512]{2,1,0:T(8,128)(2,1)}), bf16[16,128,512]{2,1,0:T(8,128)(2,1)}) %all-reduce.17.cloned.1.call-update) | async-done | bytes 2097168 | tf_op jit(solution)/shard_map/psum | solution.py:43
  726.8 1.1 fusion.18
  728.0 0.1 maximum_bitcast_fusion.1
  728.1 1.0 copy.17
  (34 shorter events, 0.4 us)
Async XLA Ops:
  7.2 51.1 %all-gather.13.cloned.1.call-start = ((), (), s32[]{:S(2)}) async-start(), calls=%async_computation.6 | async-start | bytes 2228224 | tf_op jit(solution)/shard_map/all_gather | solution.py:15
  9.0 117.6 %all-reduce.7.cloned.1.call-start = ((), (), s32[]{:S(2)}) async-start(), calls=%async_computation | async-start | bytes 2097152 | tf_op jit(solution)/shard_map/psum | solution.py:37
  58.2 68.4 %copy-start.6 = (bf16[4,1,1,128,512]{4,3,2,1,0:T(8,128)(2,1)S(1)}, bf16[4,1,1,128,512]{4,3,2,1,0:T(8,128)(2,1)}, u32[]{:S(2)}) copy-start(bf16[4,1,1,128,512]{4,3,2,1,0:T(8,128)(2,1)} %param.4) | copy-start | bytes 1572868
  58.2 68.4 %copy-start.7 = (bf16[4,1,1,1,128,128]{5,4,3,2,1,0:T(8,128)(2,1)S(1)}, bf16[4,1,1,1,128,128]{5,4,3,2,1,0:T(8,128)(2,1)}, u32[]{:S(2)}) copy-start(bf16[4,1,1,1,128,128]{5,4,3,2,1,0:T(8,128)(2,1)} %param.5) | copy-start | bytes 393220
  64.5 109.2 %all-gather.15.cloned.1.call-start = ((), (), s32[]{:S(2)}) async-start(), calls=%async_computation.7 | async-start | bytes 2228224 | tf_op jit(solution)/shard_map/all_gather | solution.py:15
  128.4 113.7 %all-reduce.9.cloned.1.call-start = ((), (), s32[]{:S(2)}) async-start(), calls=%async_computation.1 | async-start | bytes 2097152 | tf_op jit(solution)/shard_map/psum | solution.py:37
  180.0 108.5 %all-gather.17.cloned.1.call-start = ((), (), s32[]{:S(2)}) async-start(), calls=%async_computation.8 | async-start | bytes 2228224 | tf_op jit(solution)/shard_map/all_gather | solution.py:15
  243.9 113.0 %all-reduce.11.cloned.1.call-start = ((), (), s32[]{:S(2)}) async-start(), calls=%async_computation.2 | async-start | bytes 2097152 | tf_op jit(solution)/shard_map/psum | solution.py:37
  294.7 86.9 %all-gather.19.cloned.1.call-start = ((), (), s32[]{:S(2)}) async-start(), calls=%async_computation.9 | async-start | bytes 1179648 | tf_op jit(solution)/shard_map/all_gather | solution.py:23
  358.8 121.4 %all-reduce.13.cloned.1.call-start = ((), (), s32[]{:S(2)}) async-start(), calls=%async_computation.3 | async-start | bytes 4194304 | tf_op jit(solution)/shard_map/psum | solution.py:43
  381.6 98.7 %copy-start.2 = (bf16[512,128]{0,1:T(8,128)(2,1)S(1)}, bf16[512,128]{0,1:T(8,128)(2,1)}, u32[]{:S(2)}) copy-start(bf16[512,128]{0,1:T(8,128)(2,1)} %convolution_convert_fusion.4) | copy-start | bytes 393220
  387.9 117.0 %all-gather.21.cloned.1.call-start = ((), (), s32[]{:S(2)}) async-start(), calls=%async_computation.10 | async-start | bytes 1179648 | tf_op jit(solution)/shard_map/all_gather | solution.py:23
  482.0 121.4 %all-reduce.15.cloned.1.call-start = ((), (), s32[]{:S(2)}) async-start(), calls=%async_computation.4 | async-start | bytes 4194304 | tf_op jit(solution)/shard_map/psum | solution.py:43
  504.9 98.6 %copy-start.1 = (bf16[512,128]{0,1:T(8,128)(2,1)S(1)}, bf16[512,128]{0,1:T(8,128)(2,1)}, u32[]{:S(2)}) copy-start(bf16[512,128]{0,1:T(8,128)(2,1)} %convolution_convert_fusion.5) | copy-start | bytes 393220
  511.2 117.0 %all-gather.23.cloned.1.call-start = ((), (), s32[]{:S(2)}) async-start(), calls=%async_computation.11 | async-start | bytes 1179648 | tf_op jit(solution)/shard_map/all_gather | solution.py:23
  605.3 121.5 %all-reduce.17.cloned.1.call-start = ((), (), s32[]{:S(2)}) async-start(), calls=%async_computation.5 | async-start | bytes 4194304 | tf_op jit(solution)/shard_map/psum | solution.py:43
  628.1 6.3 copy-start
  628.1 99.8 %copy-start.3 = (bf16[512,128]{1,0:T(8,128)(2,1)S(1)}, bf16[512,128]{1,0:T(8,128)(2,1)}, u32[]{:S(2)}) copy-start(bf16[512,128]{1,0:T(8,128)(2,1)} %convolution_convert_fusion.9) | copy-start | bytes 393220
  628.1 99.8 %copy-start.4 = (bf16[512,128]{1,0:T(8,128)(2,1)S(1)}, bf16[512,128]{1,0:T(8,128)(2,1)}, u32[]{:S(2)}) copy-start(bf16[512,128]{1,0:T(8,128)(2,1)} %convolution_convert_fusion.8) | copy-start | bytes 393220
  628.2 99.8 %copy-start.5 = (bf16[512,128]{1,0:T(8,128)(2,1)S(1)}, bf16[512,128]{1,0:T(8,128)(2,1)}, u32[]{:S(2)}) copy-start(bf16[512,128]{1,0:T(8,128)(2,1)} %convolution_convert_fusion.7) | copy-start | bytes 393220
Sparse Core Ops, SparseCore 0:
  10.7 47.4 all-gather.12
  64.6 61.9 all-reduce.6
  129.4 44.3 all-gather.14
  180.1 61.9 all-reduce.8
  244.1 44.3 all-gather.16
  294.8 61.9 all-reduce.10
  358.9 22.6 all-gather.18
  388.0 92.1 all-reduce.12
  482.2 22.6 all-gather.20
  511.3 92.1 all-reduce.14
  605.4 22.6 all-gather.22
  634.6 92.1 all-reduce.16
where the time goes:
time: 737 us; the launch traced here: 736 us
  waiting for transfers between devices  591 us (80%)
  local copies, waits for them, and re-layouts  50 us (7%)
  matrix products  49.3 us (7%)
  other arithmetic  30.3 us (4%)
  between operations  14.3 us (2%)
    psum x3, waiting for transfers between devices, backward_sum(): summed = lax.psum(blocks.astype(jnp.bfloat16), 'row').astype(jnp.float32)  276 us
    psum x3, waiting for transfers between devices, forward_sum(): lax.psum(blocks.astype(jnp.bfloat16), ('depth', 'col')).astype(jnp.float32)  186 us
    all_gather x3, waiting for transfers between devices, lift_upward(): portion = lax.all_gather(share_in, 'row', axis=0, tiled=True)  94.9 us
    all_gather x3, waiting for transfers between devices, carry_downward(): portion = lax.all_gather(share_in, ('depth', 'col'), axis=1, tiled=True)  33.9 us
    mul x6, local copies, waits for them, and re-layouts, body(): slab.reshape(gate.shape[0], block_width, gate.shape[1], block_width)  29.7 us
    dot_general x3, local copies, waits for them, and re-layouts, carry_downward(): lax.dot_general(masked, portion.reshape(span_rows, portion.shape[-1]), ((...  19.2 us
    dot_general x3, matrix products, carry_downward(): lax.dot_general(masked, portion.reshape(span_rows, portion.shape[-1]), ((...  18.8 us
    dot_general x3, matrix products, lift_upward(): jnp.dot(masked, portion.reshape(span_rows, portion.shape[-1]), preferred_...  18.6 us
  transfers between devices with their start and end apart: 12, of which 12 were waited for; matrix products, arithmetic and copies ran while one was open for 11% of the time, Pallas kernels for 0%

commit v1 on v0

--- a/solution.py
+++ b/solution.py
@@ -1,7 +1,25 @@
+import functools
 import jax
 import jax.numpy as jnp
 from jax import lax
 from jax.sharding import PartitionSpec as P
+
+
+def group_see(x_local, comm_axis, which_dim):
+    n_axis = lax.psum(1, comm_axis)
+    value_now = sorted(((k, (k + 1) % n_axis) for k in range(n_axis)))
+    mixed_arr = x_local
+    arrivals = [mixed_arr]
+    for j in range(1, n_axis):
+        mixed_arr = lax.ppermute(mixed_arr, comm_axis, perm=value_now)
+        arrivals.insert(0, mixed_arr)
+    even = jnp.concatenate(arrivals, axis=which_dim)
+    m_next = lax.axis_index(comm_axis) + 1
+    mid_arr = jnp.roll(even, m_next * x_local.shape[which_dim], axis=which_dim)
+    return mid_arr
+
+
+_start_object = functools.partial(group_see, comm_axis="row", which_dim=0)
 
 
 def apply_inverse(inverse, vector, transposed):
@@ -12,7 +30,7 @@
 
 
 def lift_upward(masked, share_in):
-    portion = lax.all_gather(share_in, "row", axis=0, tiled=True)
+    portion = _start_object(share_in)
     span_rows = portion.shape[0] * portion.shape[2]
     return jnp.dot(
         masked, portion.reshape(span_rows, portion.shape[-1]), preferred_element_type=jnp.float32

time: 737 us -> 1000 us (1.36)
  waiting for transfers between devices: 591 us -> 850 us
  matrix products: 49.3 us -> 38.6 us
    ppermute x0 -> x45, waiting for transfers between devices: none -> 362 us  [group_see(): mixed_arr = lax.ppermute(mixed_arr, comm_axis, perm=value_now)]
    all_gather x3 -> x0, waiting for transfers between devices: 94.9 us -> none  [lift_upward(): portion = lax.all_gather(share_in, 'row', axis=0, tiled=True)]
  transfers between devices with their start and end apart: 12 -> 54, of which waited for: 12 -> 52; matrix products, arithmetic and copies ran while one was open for 11% -> 8% of each run, Pallas kernels for 0% -> 0%
where the time goes in v1:
time: 1000 us; the launch traced here: 997 us
  waiting for transfers between devices  850 us (85%)
  local copies, waits for them, and re-layouts  54.8 us (5%)
  matrix products  38.6 us (4%)
  other arithmetic  32.4 us (3%)
  between operations  14.6 us (1%)
    ppermute x45, waiting for transfers between devices, group_see(): mixed_arr = lax.ppermute(mixed_arr, comm_axis, perm=value_now)  362 us
    psum x3, waiting for transfers between devices, backward_sum(): summed = lax.psum(blocks.astype(jnp.bfloat16), 'row').astype(jnp.float32)  276 us
    psum x3, waiting for transfers between devices, forward_sum(): lax.psum(blocks.astype(jnp.bfloat16), ('depth', 'col')).astype(jnp.float32)  178 us
    all_gather x3, waiting for transfers between devices, carry_downward(): portion = lax.all_gather(share_in, ('depth', 'col'), axis=1, tiled=True)  33.8 us
    mul x6, local copies, waits for them, and re-layouts, body(): slab.reshape(gate.shape[0], block_width, gate.shape[1], block_width)  29.8 us
  transfers between devices with their start and end apart: 54, of which 52 were waited for; matrix products, arithmetic and copies ran while one was open for 8% of the time, Pallas kernels for 0%

profile of v1, /device:TPU:0, one launch (start us, length us, event | category | flops | bytes accessed | tf_op | source)
XLA Modules:
  0.0 996.8 jit_solution(14982104631491592231)
XLA Ops:
  18.2 8.3 collective-permute-done.1
  26.5 8.3 collective-permute-done.2
  34.8 8.3 collective-permute-done.3
  43.1 8.3 collective-permute-done.4
  51.4 8.9 collective-permute-done.5
  60.2 9.4 collective-permute-done.6
  69.6 8.5 collective-permute-done.7
  78.1 8.3 collective-permute-done.8
  86.4 8.3 collective-permute-done.9
  94.7 8.3 collective-permute-done.10
  103.0 8.3 collective-permute-done.11
  149.8 13.4 %slice_multiply_fusion.2 = (bf16[1,1,1024,1,2048]{4,2,3,1,0:T(8,128)(2,1)}, bf16[1,1,1024,1,2048]{4,2,3,1,0:T(8,128)(2,1)}, bf16[1,1,1024,1,2048]{4,2,3,1,0:T(8,128)(2,1)}) fusion(bf16[1,1,1024,1,2048]{4,2,3,1,0:T(8,128)(2,1)} %mul.63, bf16[3,1,1024,1,2048]{4,2,3,1,0:T(8,128)(2,1)} %param.8, bf16[1,1,1024,1,2048]{4,2,3,1,0:T(8,128)(2,1)} %mul.72, ...), kind=kLoop, calls=%fused_computation.14 | loop fusion | flops 6291456 | bytes 37748736 | tf_op jit(solution)/shard_map/mul | solution.py:75
  169.2 65.4 %all-reduce.7.cloned.1.call-done = bf16[8,128,512]{2,1,0:T(8,128)(2,1)} async-done(((bf16[8,128,512]{2,1,0:T(8,128)(2,1)}), bf16[8,128,512]{2,1,0:T(8,128)(2,1)}) %all-reduce.7.cloned.1.call-update) | async-done | bytes 1048592 | tf_op jit(solution)/shard_map/psum | solution.py:55
  244.0 8.3 collective-permute-done.16
  252.3 8.3 collective-permute-done.17
  260.6 9.1 collective-permute-done.18
  269.7 9.1 collective-permute-done.19
  278.8 8.3 collective-permute-done.20
  287.1 8.3 collective-permute-done.21
  295.4 8.3 collective-permute-done.22
  303.7 8.3 collective-permute-done.23
  312.0 8.6 collective-permute-done.24
  320.6 9.6 collective-permute-done.25
  330.2 8.8 collective-permute-done.26
  339.0 8.3 collective-permute-done.27
  347.3 8.3 collective-permute-done.28
  369.9 56.4 %all-reduce.9.cloned.1.call-done = bf16[8,128,512]{2,1,0:T(8,128)(2,1)} async-done(((bf16[8,128,512]{2,1,0:T(8,128)(2,1)}), bf16[8,128,512]{2,1,0:T(8,128)(2,1)}) %all-reduce.9.cloned.1.call-update) | async-done | bytes 1048592 | tf_op jit(solution)/shard_map/psum | solution.py:55
  435.8 8.3 collective-permute-done.31
  444.1 8.3 collective-permute-done.32
  452.3 9.1 collective-permute-done.33
  461.5 9.1 collective-permute-done.34
  470.6 8.3 collective-permute-done.35
  478.9 8.3 collective-permute-done.36
  487.2 8.3 collective-permute-done.37
  495.4 8.3 collective-permute-done.38
  503.7 8.6 collective-permute-done.39
  512.3 9.6 collective-permute-done.40
  522.0 8.8 collective-permute-done.41
  530.8 8.3 collective-permute-done.42
  539.0 8.3 collective-permute-done.43
  547.3 8.3 collective-permute-done.44
  561.5 56.4 %all-reduce.11.cloned.1.call-done = bf16[8,128,512]{2,1,0:T(8,128)(2,1)} async-done(((bf16[8,128,512]{2,1,0:T(8,128)(2,1)}), bf16[8,128,512]{2,1,0:T(8,128)(2,1)}) %all-reduce.11.cloned.1.call-update) | async-done | bytes 1048592 | tf_op jit(solution)/shard_map/psum | solution.py:55
  620.1 15.1 %fusion.2 = (bf16[2048,1024]{0,1:T(8,128)(2,1)}, bf16[2048,1024]{0,1:T(8,128)(2,1)}, bf16[2048,1024]{0,1:T(8,128)(2,1)}) fusion(bf16[128,8,16,128]{3,2,1,0:T(8,128)(2,1)} %bitcast.185, bf16[3,1,1024,1,2048]{4,2,3,1,0:T(8,128)(2,1)} %param.8, bf16[128,8,16,128]{3,2,1,0:T(8,128)(2,1)} %bitcast.186, bf16[128,8,16,128]{3,2,1,0:T(8,128)(2,1)} %bitcast.187), kind=kLoop, calls=%fused_computation.5 | loop fusion | flops 6291456 | bytes 37748736 | tf_op jit(solution)/shard_map/dot_general | solution.py:43
  649.0 92.3 %all-reduce.13.cloned.1.call-done = bf16[16,128,512]{2,1,0:T(8,128)(2,1)} async-done(((bf16[16,128,512]{2,1,0:T(8,128)(2,1)}), bf16[16,128,512]{2,1,0:T(8,128)(2,1)}) %all-reduce.13.cloned.1.call-update) | async-done | bytes 2097168 | tf_op jit(solution)/shard_map/psum | solution.py:61
  749.5 16.4 %all-gather.9.cloned.1.call-done = bf16[1024,512]{0,1:T(8,128)(2,1)} async-done(((bf16[128,512]{0,1:T(8,128)(2,1)}), bf16[1024,512]{0,1:T(8,128)(2,1)}) %all-gather.9.cloned.1.call-update) | async-done | bytes 1048592 | tf_op jit(solution)/shard_map/all_gather | solution.py:41
  772.2 92.3 %all-reduce.15.cloned.1.call-done = bf16[16,128,512]{2,1,0:T(8,128)(2,1)} async-done(((bf16[16,128,512]{2,1,0:T(8,128)(2,1)}), bf16[16,128,512]{2,1,0:T(8,128)(2,1)}) %all-reduce.15.cloned.1.call-update) | async-done | bytes 2097168 | tf_op jit(solution)/shard_map/psum | solution.py:61
  872.8 16.4 %all-gather.11.cloned.1.call-done = bf16[1024,512]{0,1:T(8,128)(2,1)} async-done(((bf16[128,512]{0,1:T(8,128)(2,1)}), bf16[1024,512]{0,1:T(8,128)(2,1)}) %all-gather.11.cloned.1.call-update) | async-done | bytes 1048592 | tf_op jit(solution)/shard_map/all_gather | solution.py:41
  896.3 91.5 %all-reduce.17.cloned.1.call-done = bf16[16,128,512]{2,1,0:T(8,128)(2,1)} async-done(((bf16[16,128,512]{2,1,0:T(8,128)(2,1)}), bf16[16,128,512]{2,1,0:T(8,128)(2,1)}) %all-reduce.17.cloned.1.call-update) | async-done | bytes 2097168 | tf_op jit(solution)/shard_map/psum | solution.py:61
  (166 shorter events, 142.3 us)
Async XLA Ops:
  7.2 227.4 %all-reduce.7.cloned.1.call-start = ((), (), s32[]{:S(2)}) async-start(), calls=%async_computation | async-start | bytes 2097152 | tf_op jit(solution)/shard_map/psum | solution.py:55
  8.3 9.9 collective-permute-start
  18.2 8.3 collective-permute-start.1
  26.5 8.3 collective-permute-start.2
  34.8 8.3 collective-permute-start.3
  43.1 8.3 collective-permute-start.4
  51.4 8.9 collective-permute-start.5
  60.2 9.4 collective-permute-start.6
  69.6 8.5 collective-permute-start.7
  78.1 8.3 collective-permute-start.8
  86.4 8.3 collective-permute-start.9
  94.7 8.3 collective-permute-start.10
  103.0 8.3 collective-permute-start.11
  111.3 8.3 collective-permute-start.12
  119.6 29.8 %collective-permute-start.13 = (bf16[1,1,128,512]{3,2,1,0:T(8,128)(2,1)S(1)}, bf16[1,1,128,512]{3,2,1,0:T(8,128)(2,1)S(1)}, u32[]{:S(2)}, u32[]{:S(2)}) collective-permute-start(bf16[1,1,128,512]{3,2,1,0:T(8,128)(2,1)S(1)} %collective-permute-done.12), channel_id=1, source_target_pairs={{0,4},{4,8},{8,12},{12,16},{16,20},{20,24},{24,28},{28,32},{32,36}... | collective-permute-start | bytes 393224 | tf_op jit(solution)/shard_map/ppermute | solution.py:14
  149.4 13.9 %collective-permute-start.14 = (bf16[1,1,128,512]{3,2,1,0:T(8,128)(2,1)S(1)}, bf16[1,1,128,512]{3,2,1,0:T(8,128)(2,1)S(1)}, u32[]{:S(2)}, u32[]{:S(2)}) collective-permute-start(bf16[1,1,128,512]{3,2,1,0:T(8,128)(2,1)S(1)} %collective-permute-done.13), channel_id=1, source_target_pairs={{0,4},{4,8},{8,12},{12,16},{16,20},{20,24},{24,28},{28,32},{32,36}... | collective-permute-start | bytes 393224 | tf_op jit(solution)/shard_map/ppermute | solution.py:14
  169.1 257.2 %all-reduce.9.cloned.1.call-start = ((), (), s32[]{:S(2)}) async-start(), calls=%async_computation.1 | async-start | bytes 2097152 | tf_op jit(solution)/shard_map/psum | solution.py:55
  235.7 8.4 collective-permute-start.15
  260.6 9.1 collective-permute-start.18
  269.7 9.1 collective-permute-start.19
  278.8 8.3 collective-permute-start.20
  287.1 8.3 collective-permute-start.21
  295.4 8.3 collective-permute-start.22
  303.7 8.3 collective-permute-start.23
  312.0 8.6 collective-permute-start.24
  320.6 9.7 collective-permute-start.25
  330.2 8.8 collective-permute-start.26
  339.0 8.3 collective-permute-start.27
  355.6 8.4 collective-permute-start.29
  369.9 248.0 %all-reduce.11.cloned.1.call-start = ((), (), s32[]{:S(2)}) async-start(), calls=%async_computation.2 | async-start | bytes 2097152 | tf_op jit(solution)/shard_map/psum | solution.py:55
  427.4 8.4 collective-permute-start.30
  435.8 8.3 collective-permute-start.31
  444.1 8.3 collective-permute-start.32
  452.3 9.1 collective-permute-start.33
  461.5 9.1 collective-permute-start.34
  478.9 8.3 collective-permute-start.36
  487.2 8.3 collective-permute-start.37
  495.4 8.3 collective-permute-start.38
  503.7 8.6 collective-permute-start.39
  512.3 9.6 collective-permute-start.40
  522.0 8.8 collective-permute-start.41
  530.8 8.3 collective-permute-start.42
  561.4 81.2 %all-gather.7.cloned.1.call-start = ((), (), s32[]{:S(2)}) async-start(), calls=%async_computation.6 | async-start | bytes 1179648 | tf_op jit(solution)/shard_map/all_gather | solution.py:41
  619.9 121.4 %all-reduce.13.cloned.1.call-start = ((), (), s32[]{:S(2)}) async-start(), calls=%async_computation.3 | async-start | bytes 4194304 | tf_op jit(solution)/shard_map/psum | solution.py:61
  648.9 117.0 %all-gather.9.cloned.1.call-start = ((), (), s32[]{:S(2)}) async-start(), calls=%async_computation.7 | async-start | bytes 1179648 | tf_op jit(solution)/shard_map/all_gather | solution.py:41
  743.1 121.5 %all-reduce.15.cloned.1.call-start = ((), (), s32[]{:S(2)}) async-start(), calls=%async_computation.4 | async-start | bytes 4194304 | tf_op jit(solution)/shard_map/psum | solution.py:61
  772.2 117.0 %all-gather.11.cloned.1.call-start = ((), (), s32[]{:S(2)}) async-start(), calls=%async_computation.8 | async-start | bytes 1179648 | tf_op jit(solution)/shard_map/all_gather | solution.py:41
  866.4 121.5 %all-reduce.17.cloned.1.call-start = ((), (), s32[]{:S(2)}) async-start(), calls=%async_computation.5 | async-start | bytes 4194304 | tf_op jit(solution)/shard_map/psum | solution.py:61
  (14 other events, 474.5 us)
Sparse Core Ops, SparseCore 0:
  169.2 65.2 all-reduce.6
  370.0 56.2 all-reduce.8
  561.6 56.2 all-reduce.10
  620.0 22.6 all-gather.6
  649.0 92.1 all-reduce.12
  743.2 22.6 all-gather.8
  772.3 92.1 all-reduce.14
  866.5 22.6 all-gather.10
  895.6 92.1 all-reduce.16
